TPU v7x, 256 devices: a whole 4x4x8 slice. The times are simulated.
256 devices in a mesh: dp: 8 (over x, core), expert: 32 (over z, y).
Axes of the slice: x: 4, y: 4, z: 8, core: 2. Of those that a mesh axis runs over, the one named last changes fastest.
Arguments:
- tokens: bfloat16 [5120, 262144], P(None, ('dp', 'expert')), may hold values from -24 to 24, as said below
- router: bfloat16 [5120, 160], P(None, 'expert'), may hold values from -1 to 1, as said below
- device_pick: int32 [3, 262144], P(None, 'dp'), may hold values from 0 to 31, as said below
- expert_pick: int32 [6, 262144], P(None, 'dp'), may hold values from 0 to 159, as said below
Outputs:
- gates: float32 [6, 262144], P(None, 'dp')
- device_max: float32 [32, 262144], P('expert', 'dp')
- balance: float32 [3], replicated
Inputs may be any that keep to these rules, and one draw needn't show every extreme that they name: tokens lie within the range; in each column the values are of order one, except in a few columns. router entries are of order 1 / sqrt(5120). `device_pick`: each column names 3 different devices. `expert_pick`: each column names 6 different experts, two on each device of the column's device_pick, in that order; the device of expert e is e // 5.
All inputs are finite; a program needn't handle non-finite values.
Results may differ from a plain program's by a relative error of at most 0.0003.
Values may be sent and summed in bfloat16 or wider, within the bound.
No kernel may reach another device: no remote copies, remote signals or barrier semaphores. Data moves between devices by JAX's collectives and lax.ppermute only.
A program may use at most 64 MiB of HBM per device.

v0:
```python
import jax
import jax.numpy as jnp
from jax import lax
from jax.sharding import Mesh
from jax.sharding import PartitionSpec as P

TOP = 6
DEV_TOP = 3
EXPERT = ("expert_0", "expert_1")
DP = ("dp_0", "dp_1")
DP_EXPERT = ("dp_0", "dp_1", "expert_0", "expert_1")


def gathered_by_axis(x, axes, dim):
    for axis in reversed(axes):
        x = lax.all_gather(x, axis, axis=dim, tiled=True)
    return x


def joined_along(tiles, dim):
    shape = list(tiles.shape[1:])
    shape[dim] *= tiles.shape[0]
    return jnp.moveaxis(tiles, 0, dim).reshape(shape)


def sent_to_all(x, axis):
    length = lax.axis_size(axis)
    return lax.all_to_all(jnp.broadcast_to(x[None], (length, *x.shape)), axis, 0, 0, tiled=True)


def gathered_copies(x, axis, dim):
    return joined_along(sent_to_all(x, axis), dim)


def by_axis(x, axes):
    for axis in axes:
        x = lax.psum(x, axis)
    return x


def local(tokens, router, device_pick, expert_pick):
    share = tokens.shape[1]
    num_devices = lax.axis_size(EXPERT)
    per_device = router.shape[1]
    num_experts = per_device * num_devices
    tok_rows = share * num_devices
    my_index = lax.axis_index(EXPERT)
    total_tokens = tok_rows * lax.axis_size(DP)
    scores = jnp.dot(
        tokens.T, gathered_by_axis(router, EXPERT, 1), preferred_element_type=jnp.float32
    ).T
    peak = jnp.max(scores, axis=0, keepdims=True)
    raised = jnp.exp(scores - peak)
    probs = raised / jnp.sum(raised, axis=0, keepdims=True)
    first_col = my_index * share
    experts_here = lax.dynamic_slice_in_dim(expert_pick, first_col, share, 1)
    devices_here = lax.dynamic_slice_in_dim(device_pick, first_col, share, 1)
    col_gates = jnp.take_along_axis(probs, experts_here, axis=0)
    col_maxima = jnp.max(probs.reshape(num_devices, per_device, share), axis=1)
    gates = gathered_copies(col_gates, EXPERT, 1)
    device_max = lax.all_to_all(col_maxima, EXPERT, split_axis=0, concat_axis=1, tiled=True)
    prob_sum = jnp.sum(probs, axis=1)
    all_ids = jnp.arange(num_experts, dtype=jnp.int32)
    counts = jnp.sum(
        (all_ids[:, None, None] == experts_here[None, :, :]).astype(jnp.float32), axis=(1, 2)
    )
    dev_ids = jnp.arange(num_devices, dtype=jnp.int32)
    sent_counts = jnp.sum(
        (dev_ids[:, None, None] == devices_here[None, :, :]).astype(jnp.float32), axis=(1, 2)
    )
    prob_sum, counts, sent_counts = (
        by_axis(prob_sum, DP_EXPERT),
        by_axis(counts, DP_EXPERT),
        by_axis(sent_counts, DP_EXPERT),
    )
    freq = counts * (num_experts / (TOP * total_tokens))
    prob = prob_sum / total_tokens
    dev_freq = jnp.mean(freq.reshape(num_devices, per_device), axis=1)
    dev_prob = jnp.sum(prob.reshape(num_devices, per_device), axis=1)
    sent = sent_counts * (num_devices / (DEV_TOP * total_tokens))
    balance = jnp.stack(
        [jnp.sum(freq * prob), jnp.sum(dev_freq * dev_prob), jnp.sum(sent * dev_prob)]
    )
    return (gates, device_max, balance)


def solution(mesh):
    torus = Mesh(mesh.devices.reshape(4, 2, 8, 4), ("dp_0", "dp_1", "expert_0", "expert_1"))
    return jax.shard_map(
        local,
        mesh=torus,
        in_specs=(P(None, DP_EXPERT), P(None, EXPERT), P(None, DP), P(None, DP)),
        out_specs=(P(None, DP), P(EXPERT, DP), P()),
        check_vma=False,
    )
```

profile of v0, /device:TPU:2, one launch (start us, length us, event | category | flops | bytes accessed | tf_op | source)
XLA Modules:
  0.0 194.9 jit_solution(3939025640600472953)
XLA Ops:
  7.2 13.3 %all-gather = bf16[4,5,5120]{2,1,0:T(8,128)(2,1)S(1)} all-gather(bf16[1,5,5120]{2,1,0:T(8,128)(2,1)} %bitcast.18), channel_id=1, replica_groups=mesh['dp_0'=4,'dp_1'=2,'expert_0'=8,'expert_1'=4] {'expert_1'}, dimensions={0}, use_global_device_ids=true | all-gather | bytes 256000 | tf_op jit(solution)/shard_map/all_gather | solution.py:16
  20.5 0.8 reshape.59
  21.3 43.4 %all-gather.4.cloned.1.call-done = bf16[8,20,5120]{2,1,0:T(8,128)(2,1)} async-done(((bf16[1,20,5120]{2,1,0:T(8,128)(2,1)}), bf16[8,20,5120]{2,1,0:T(8,128)(2,1)}) %all-gather.4.cloned.1.call-update) | async-done | bytes 1638416 | tf_op jit(solution)/shard_map/all_gather | solution.py:16
  64.7 1.7 reshape.60
  66.4 5.8 %fusion.4 = (f32[1024]{0:T(1024)S(1)}, f32[160,1024]{1,0:T(8,128)S(1)}) fusion(bf16[160,5120]{1,0:T(8,128)(2,1)S(1)} %reshape.60, bf16[5120,1024]{1,0:T(8,128)(2,1)} %param.4), kind=kOutput, calls=%fused_computation.20 | convolution fusion | flops 1677884416 | bytes 12783616 | tf_op jit(solution)/shard_map/dot_general | solution.py:49
  72.4 0.2 fusion.2
  72.7 0.3 reduce_max.19
  73.0 0.7 all_to_all.16
  73.7 7.0 %all-to-all-start.1 = ((f32[32,1,1024]{2,1,0:T(1,128)}), f32[32,1,1024]{2,1,0:T(1,128)S(1)}, u32[]{:S(2)}, u32[]{:S(2)}) async-start(f32[32,1,1024]{2,1,0:T(1,128)} %all_to_all.16), calls=%async_computation.1 | async-start | bytes 262144 | tf_op jit(solution)/shard_map/all_to_all | solution.py:61
  80.8 0.8 bitcast_or_fusion
  81.6 49.3 %gather_fusion = f32[6144]{0:T(1024)S(1)} fusion(f32[160,1024]{1,0:T(8,128)S(1)} %get-tuple-element.18, s32[6144]{0:T(1024)S(1)} %reshape.46), kind=kCustom, calls=%fused_computation | custom fusion | bytes 98304 | tf_op jit(solution)/shard_map/jit(take_along_axis)/gather | solution.py:58
  130.9 1.1 broadcast_in_dim.7
  132.0 9.8 %all-to-all-start = ((f32[32,6,1024]{2,1,0:T(8,128)}), f32[32,6,1024]{2,1,0:T(8,128)S(1)}, u32[]{:S(2)}, u32[]{:S(2)}) async-start(f32[32,6,1024]{2,1,0:T(8,128)} %broadcast_in_dim.7), calls=%async_computation | async-start | bytes 2097152 | tf_op jit(solution)/shard_map/all_to_all | solution.py:28
  141.8 0.2 convert_reduce_fusion.1
  142.0 0.6 convert_reduce_fusion
  142.5 8.6 %all-reduce.2 = (f32[160]{0:T(256)S(1)}, f32[160]{0:T(256)S(1)}, f32[32]{0:T(128)S(1)}) all-reduce(f32[160]{0:T(256)S(1)} %get-tuple-element.17, f32[160]{0:T(256)S(1)} %convert_reduce_fusion, f32[32]{0:T(128)S(1)} %convert_reduce_fusion.1), channel_id=1, replica_groups=mesh['dp_0'=4,'dp_1'=2,'expert_0'=8,'expert_1'=4] {'dp_0'}, use_global_device_ids=true, to_apply=%region_9.10 | all-reduce | flops 352 | bytes 2816 | tf_op jit(solution)/shard_map/psum | solution.py:37
  151.1 2.5 %all-reduce.3 = (f32[160]{0:T(256)S(1)}, f32[160]{0:T(256)S(1)}, f32[32]{0:T(128)S(1)}) all-reduce(f32[160]{0:T(256)S(1)} %get-tuple-element.11, f32[160]{0:T(256)S(1)} %get-tuple-element.12, f32[32]{0:T(128)S(1)} %get-tuple-element.13), channel_id=1, replica_groups=mesh['dp_0'=4,'dp_1'=2,'expert_0'=8,'expert_1'=4] {'dp_1'}, use_global_device_ids=true, to_apply=%region_10.11 | all-reduce | flops 352 | bytes 2816 | tf_op jit(solution)/shard_map/psum | solution.py:37
  153.6 18.1 %all-reduce = (f32[160]{0:T(256)S(1)}, f32[160]{0:T(256)S(1)}, f32[32]{0:T(128)S(1)}) all-reduce(f32[160]{0:T(256)S(1)} %get-tuple-element.14, f32[160]{0:T(256)S(1)} %get-tuple-element.15, f32[32]{0:T(128)S(1)} %get-tuple-element.16), channel_id=1, replica_groups=mesh['dp_0'=4,'dp_1'=2,'expert_0'=8,'expert_1'=4] {'expert_0'}, use_global_device_ids=true, to_apply=%region_11.12 | all-reduce | flops 352 | bytes 2816 | tf_op jit(solution)/shard_map/psum | solution.py:37
  171.7 10.5 %all-reduce.1 = (f32[160]{0:T(256)S(1)}, f32[160]{0:T(256)S(1)}, f32[32]{0:T(128)S(1)}) all-reduce(f32[160]{0:T(256)S(1)} %get-tuple-element.5, f32[160]{0:T(256)S(1)} %get-tuple-element.6, f32[32]{0:T(128)S(1)} %get-tuple-element.7), channel_id=1, replica_groups=mesh['dp_0'=4,'dp_1'=2,'expert_0'=8,'expert_1'=4] {'expert_1'}, use_global_device_ids=true, to_apply=%region_12.13 | all-reduce | flops 352 | bytes 2816 | tf_op jit(solution)/shard_map/psum | solution.py:37
  182.2 0.6 multiply_reduce_fusion
  183.3 0.7 multiply_reduce_fusion.2
  184.0 2.5 %pad_maximum_fusion = f32[3]{0:T(128)} fusion(f32[1]{0:T(128)} %bitcast.8, f32[1]{0:T(128)} %bitcast.7, f32[1]{0:T(128)} %bitcast.6), kind=kLoop, calls=%fused_computation.12 | loop fusion | flops 6 | bytes 24 | tf_op jit(solution)/shard_map/stack | solution.py:81
  186.4 1.0 copy.9
  187.4 0.7 copy.10
  (16 shorter events, 0.7 us)
Async XLA Ops:
  7.2 134.6 %copy-start = (s32[3,32768]{1,0:T(4,128)S(1)}, s32[3,32768]{1,0:T(4,128)}, u32[]{:S(2)}) copy-start(s32[3,32768]{1,0:T(4,128)} %param.6) | copy-start | bytes 1179652
  7.2 57.5 %all-gather.4.cloned.1.call-start = ((), (), s32[]{:S(2)}) async-start(), calls=%async_computation.2 | async-start | bytes 2211840 | tf_op jit(solution)/shard_map/all_gather | solution.py:16
  73.7 57.2 %all-to-all-start.1 = ((f32[32,1,1024]{2,1,0:T(1,128)}), f32[32,1,1024]{2,1,0:T(1,128)S(1)}, u32[]{:S(2)}, u32[]{:S(2)}) async-start(f32[32,1,1024]{2,1,0:T(1,128)} %all_to_all.16), calls=%async_computation.1 | async-start | bytes 262144 | tf_op jit(solution)/shard_map/all_to_all | solution.py:61
  132.0 54.4 %all-to-all-start = ((f32[32,6,1024]{2,1,0:T(8,128)}), f32[32,6,1024]{2,1,0:T(8,128)S(1)}, u32[]{:S(2)}, u32[]{:S(2)}) async-start(f32[32,6,1024]{2,1,0:T(8,128)} %broadcast_in_dim.7), calls=%async_computation | async-start | bytes 2097152 | tf_op jit(solution)/shard_map/all_to_all | solution.py:28
Sparse Core Ops, SparseCore 0:
  21.4 43.2 all-gather.3
where the time goes:
time: 195 us
  local copies, waits for them, and re-layouts  55.6 us (29%)
  blocking collectives  52.9 us (27%)
  waiting for transfers between devices  43.4 us (22%)
  starting transfers between devices  16.8 us (9%)
  between operations  14.2 us (7%)
  other arithmetic  6.14 us (3%)
  matrix products  5.84 us (3%)
    gather x3, local copies, waits for them, and re-layouts, local(): col_gates = jnp.take_along_axis(probs, experts_here, axis=0)  49.3 us
    all_gather x1, waiting for transfers between devices, gathered_by_axis(): x = lax.all_gather(x, axis, axis=dim, tiled=True)  43.4 us
    psum x4, blocking collectives, by_axis(): x = lax.psum(x, axis)  39.7 us
    all_gather x1, blocking collectives, gathered_by_axis(): x = lax.all_gather(x, axis, axis=dim, tiled=True)  13.3 us
    all_to_all x1, starting transfers between devices, sent_to_all(): lax.all_to_all(jnp.broadcast_to(x[None], (length, *x.shape)), axis, 0, 0,...  9.78 us
    all_to_all x1, starting transfers between devices, local(): lax.all_to_all(col_maxima, EXPERT, split_axis=0, concat_axis=1, tiled=True)  7.02 us
    dot_general x1, matrix products, local(): jnp.dot(tokens.T, gathered_by_axis(router, EXPERT, 1), preferred_element_...  5.84 us
    unnamed x6, local copies, waits for them, and re-layouts  4.1 us
  transfers between devices with their start and end apart: 3, of which 1 were waited for; matrix products, arithmetic and copies ran while one was open for 28% of the time, Pallas kernels for 0%

commit v1 on v0

--- a/solution.py
+++ b/solution.py
@@ -34,7 +34,7 @@
 
 def by_axis(x, axes):
     for axis in axes:
-        x = lax.psum(x, axis)
+        x = jnp.sum(lax.all_gather(x, axis), axis=0)
     return x
 
 

time: 195 us -> 219 us (1.12)
  blocking collectives: 52.9 us -> 65 us
  local copies, waits for them, and re-layouts: 55.6 us -> 61.9 us
  between operations: 14.2 us -> 19.3 us
    unnamed x0 -> x4, blocking collectives: none -> 51.8 us
    psum x4 -> x0, blocking collectives: 39.7 us -> none  [by_axis(): x = lax.psum(x, axis)]
    unnamed x6 -> x42, local copies, waits for them, and re-layouts: 4.1 us -> 9.48 us
where the time goes in v1:
time: 219 us
  blocking collectives  65 us (30%)
  local copies, waits for them, and re-layouts  61.9 us (28%)
  waiting for transfers between devices  43.4 us (20%)
  between operations  19.3 us (9%)
  starting transfers between devices  16.8 us (8%)
  other arithmetic  6.38 us (3%)
  matrix products  5.84 us (3%)
    unnamed x4, blocking collectives  51.8 us
    gather x3, local copies, waits for them, and re-layouts, local(): col_gates = jnp.take_along_axis(probs, experts_here, axis=0)  49.3 us
    all_gather x1, waiting for transfers between devices, gathered_by_axis(): x = lax.all_gather(x, axis, axis=dim, tiled=True)  43.4 us
    all_gather x1, blocking collectives, gathered_by_axis(): x = lax.all_gather(x, axis, axis=dim, tiled=True)  13.3 us
    all_to_all x1, starting transfers between devices, sent_to_all(): lax.all_to_all(jnp.broadcast_to(x[None], (length, *x.shape)), axis, 0, 0,...  9.78 us
    unnamed x42, local copies, waits for them, and re-layouts  9.48 us
    all_to_all x1, starting transfers between devices, local(): lax.all_to_all(col_maxima, EXPERT, split_axis=0, concat_axis=1, tiled=True)  7.02 us
    dot_general x1, matrix products, local(): jnp.dot(tokens.T, gathered_by_axis(router, EXPERT, 1), preferred_element_...  5.84 us
  transfers between devices with their start and end apart: 3, of which 1 were waited for; matrix products, arithmetic and copies ran while one was open for 28% of the time, Pallas kernels for 0%

profile of v1, /device:TPU:2, one launch (start us, length us, event | category | flops | bytes accessed | tf_op | source)
XLA Modules:
  0.0 218.7 jit_solution(9161955696908991325)
XLA Ops:
  7.2 13.3 %all-gather.12 = bf16[4,5,5120]{2,1,0:T(8,128)(2,1)S(1)} all-gather(bf16[1,5,5120]{2,1,0:T(8,128)(2,1)} %bitcast.26), channel_id=1, replica_groups=mesh['dp_0'=4,'dp_1'=2,'expert_0'=8,'expert_1'=4] {'expert_1'}, dimensions={0}, use_global_device_ids=true | all-gather | bytes 256000 | tf_op jit(solution)/shard_map/all_gather | solution.py:16
  20.5 0.8 reshape.107
  21.3 43.4 %all-gather.16.cloned.1.call-done = bf16[8,20,5120]{2,1,0:T(8,128)(2,1)} async-done(((bf16[1,20,5120]{2,1,0:T(8,128)(2,1)}), bf16[8,20,5120]{2,1,0:T(8,128)(2,1)}) %all-gather.16.cloned.1.call-update) | async-done | bytes 1638416 | tf_op jit(solution)/shard_map/all_gather | solution.py:16
  64.7 1.7 reshape.108
  66.4 5.8 %fusion.4 = (f32[1024]{0:T(1024)S(1)}, f32[160,1024]{1,0:T(8,128)S(1)}) fusion(bf16[160,5120]{1,0:T(8,128)(2,1)S(1)} %reshape.108, bf16[5120,1024]{1,0:T(8,128)(2,1)} %param.4), kind=kOutput, calls=%fused_computation.20 | convolution fusion | flops 1677884416 | bytes 12783616 | tf_op jit(solution)/shard_map/dot_general | solution.py:49
  73.0 0.7 all_to_all.16
  73.7 7.0 %all-to-all-start.1 = ((f32[32,1,1024]{2,1,0:T(1,128)}), f32[32,1,1024]{2,1,0:T(1,128)S(1)}, u32[]{:S(2)}, u32[]{:S(2)}) async-start(f32[32,1,1024]{2,1,0:T(1,128)} %all_to_all.16), calls=%async_computation.1 | async-start | bytes 262144 | tf_op jit(solution)/shard_map/all_to_all | solution.py:61
  80.8 0.8 bitcast_or_fusion
  81.6 49.3 %gather_fusion = f32[6144]{0:T(1024)S(1)} fusion(f32[160,1024]{1,0:T(8,128)S(1)} %get-tuple-element.18, s32[6144]{0:T(1024)S(1)} %reshape.46), kind=kCustom, calls=%fused_computation | custom fusion | bytes 98304 | tf_op jit(solution)/shard_map/jit(take_along_axis)/gather | solution.py:58
  131.0 1.1 broadcast_in_dim.7
  132.1 9.8 %all-to-all-start = ((f32[32,6,1024]{2,1,0:T(8,128)}), f32[32,6,1024]{2,1,0:T(8,128)S(1)}, u32[]{:S(2)}, u32[]{:S(2)}) async-start(f32[32,6,1024]{2,1,0:T(8,128)} %broadcast_in_dim.7), calls=%async_computation | async-start | bytes 2097152 | tf_op jit(solution)/shard_map/all_to_all | solution.py:28
  141.9 0.6 dynamic-slice
  143.8 0.7 dynamic-slice.1
  145.7 0.6 dynamic-slice.2
  147.5 0.6 dynamic-slice.3
  150.8 8.8 %all-reduce.14 = (f32[640]{0:T(1024)S(1)}, f32[640]{0:T(1024)S(1)}, f32[128]{0:T(128)S(1)}) all-reduce(f32[640]{0:T(1024)S(1)} %dynamic-update-slice.4, f32[640]{0:T(1024)S(1)} %dynamic-update-slice, f32[128]{0:T(128)S(1)} %dynamic-update-slice.8), channel_id=6, replica_groups=mesh['dp_0'=4,'dp_1'=2,'expert_0'=8,'expert_1'=4] {'dp_0'}, use_global_device_ids=true, to_apply=%add.4 | all-reduce | flops 1408 | bytes 11264
  160.6 2.5 %all-reduce.15 = (f32[320]{0:T(512)S(1)}, f32[320]{0:T(512)S(1)}, f32[64]{0:T(128)S(1)}) all-reduce(f32[320]{0:T(512)S(1)} %dynamic-update-slice.5, f32[320]{0:T(512)S(1)} %dynamic-update-slice.1, f32[64]{0:T(128)S(1)} %dynamic-update-slice.9), channel_id=7, replica_groups=mesh['dp_0'=4,'dp_1'=2,'expert_0'=8,'expert_1'=4] {'dp_1'}, use_global_device_ids=true, to_apply=%add.5 | all-reduce | flops 704 | bytes 5632
  164.2 29.9 %all-reduce.12 = (f32[1280]{0:T(1024)S(1)}, f32[1280]{0:T(1024)S(1)}, f32[256]{0:T(256)S(1)}) all-reduce(f32[1280]{0:T(1024)S(1)} %dynamic-update-slice.6, f32[1280]{0:T(1024)S(1)} %dynamic-update-slice.2, f32[256]{0:T(256)S(1)} %dynamic-update-slice.10), channel_id=8, replica_groups=mesh['dp_0'=4,'dp_1'=2,'expert_0'=8,'expert_1'=4] {'expert_0'}, use_global_device_ids=true, to_apply=%add.6 | all-reduce | flops 2816 | bytes 22528
  195.1 10.6 %all-reduce.13 = (f32[640]{0:T(1024)S(1)}, f32[640]{0:T(1024)S(1)}, f32[128]{0:T(128)S(1)}) all-reduce(f32[640]{0:T(1024)S(1)} %dynamic-update-slice.7, f32[640]{0:T(1024)S(1)} %dynamic-update-slice.3, f32[128]{0:T(128)S(1)} %dynamic-update-slice.11), channel_id=9, replica_groups=mesh['dp_0'=4,'dp_1'=2,'expert_0'=8,'expert_1'=4] {'expert_1'}, use_global_device_ids=true, to_apply=%add.7 | all-reduce | flops 1408 | bytes 11264
  205.9 0.6 multiply_reduce_fusion
  207.1 0.7 multiply_reduce_fusion.2
  207.8 2.5 %pad_maximum_fusion = f32[3]{0:T(128)} fusion(f32[1]{0:T(128)} %bitcast.16, f32[1]{0:T(128)} %bitcast.11, f32[1]{0:T(128)} %bitcast.10), kind=kLoop, calls=%fused_computation.12 | loop fusion | flops 6 | bytes 24 | tf_op jit(solution)/shard_map/stack | solution.py:81
  210.3 1.0 copy.35
  211.2 0.7 copy.36
  (76 shorter events, 6.1 us)
Async XLA Ops:
  7.2 143.0 %copy-start = (s32[3,32768]{1,0:T(4,128)S(1)}, s32[3,32768]{1,0:T(4,128)}, u32[]{:S(2)}) copy-start(s32[3,32768]{1,0:T(4,128)} %param.6) | copy-start | bytes 1179652
  7.2 57.5 %all-gather.16.cloned.1.call-start = ((), (), s32[]{:S(2)}) async-start(), calls=%async_computation.2 | async-start | bytes 2211840 | tf_op jit(solution)/shard_map/all_gather | solution.py:16
  73.7 57.2 %all-to-all-start.1 = ((f32[32,1,1024]{2,1,0:T(1,128)}), f32[32,1,1024]{2,1,0:T(1,128)S(1)}, u32[]{:S(2)}, u32[]{:S(2)}) async-start(f32[32,1,1024]{2,1,0:T(1,128)} %all_to_all.16), calls=%async_computation.1 | async-start | bytes 262144 | tf_op jit(solution)/shard_map/all_to_all | solution.py:61
  130.9 11.0 %copy-start.4 = (u32[256]{0:T(256)S(1)}, u32[256]{0:T(256)}, u32[]{:S(2)}) copy-start(u32[256]{0:T(256)} %constant.62) | copy-start | bytes 3076
  130.9 12.9 %copy-start.3 = (u32[256]{0:T(256)S(1)}, u32[256]{0:T(256)}, u32[]{:S(2)}) copy-start(u32[256]{0:T(256)} %constant.67) | copy-start | bytes 3076
  130.9 14.8 %copy-start.2 = (u32[256]{0:T(256)S(1)}, u32[256]{0:T(256)}, u32[]{:S(2)}) copy-start(u32[256]{0:T(256)} %constant.72) | copy-start | bytes 3076
  130.9 16.6 %copy-start.1 = (u32[256]{0:T(256)S(1)}, u32[256]{0:T(256)}, u32[]{:S(2)}) copy-start(u32[256]{0:T(256)} %constant.77) | copy-start | bytes 3076
  132.1 78.2 %all-to-all-start = ((f32[32,6,1024]{2,1,0:T(8,128)}), f32[32,6,1024]{2,1,0:T(8,128)S(1)}, u32[]{:S(2)}, u32[]{:S(2)}) async-start(f32[32,6,1024]{2,1,0:T(8,128)} %broadcast_in_dim.7), calls=%async_computation | async-start | bytes 2097152 | tf_op jit(solution)/shard_map/all_to_all | solution.py:28
Sparse Core Ops, SparseCore 0:
  21.4 43.2 all-gather.15
